TPU v7x, 32 devices: a whole 2x2x4 slice. The times are simulated.
32 devices in a mesh: section: 4 (over y, x), mp: 4 (over z), dp: 2 (over core).
Axes of the slice: x: 2, y: 2, z: 4, core: 2. Of those that a mesh axis runs over, the one named last changes fastest.
Arguments:
- stream: bfloat16 [4, 64, 4096], P('dp', None, 'mp'), may hold values from -6 to 6
- cotangent: bfloat16 [4, 64, 4096], P('dp', None, 'mp'), may hold values from -6 to 6
- token_ids: int32 [4, 64], P('dp'), may hold values from 0 to 32127, as said below
- buckets: int32 [64, 64], replicated, may hold values from 0 to 31, as said below
- bias_table: float32 [32, 32], P(None, 'mp'), may hold values from -300 to 300
- gain: float32 [4, 4096], P('section'), may hold values from 0.25 to 1.75
- w_query: bfloat16 [4, 4096, 2048], P('section', None, 'mp'), may hold values from -0.01171875 to 0.01171875
- w_key: bfloat16 [4, 4096, 2048], P('section', None, 'mp'), may hold values from -0.09375 to 0.09375
- w_value: bfloat16 [4, 4096, 2048], P('section', None, 'mp'), may hold values from -0.09375 to 0.09375
- w_out: bfloat16 [4, 2048, 4096], P('section', None, 'mp'), may hold values from -0.125 to 0.125
Outputs:
- input_grads: bfloat16 [4, 4, 64, 4096], P('section', 'dp', None, 'mp')
- gain_grad: float32 [4, 4096], P('section', 'mp')
- table_grad: float32 [32, 32], P(None, 'mp')
Inputs may be any that keep to these rules, and one draw needn't show every extreme that they name: `token_ids`: in each sequence the ids are nonzero up to a length of 32 or more and zero after it. `buckets`: the bucket of a query and a key depends only on the key's position minus the query's: below 16 for keys at or before the query, 16 or more for keys after it.
All inputs are finite; a program needn't handle non-finite values.
Results may differ from a plain program's by a relative error of at most 0.035.
Values may be sent and summed in bfloat16 or wider, within the bound.
A program may use at most 64 MiB of HBM per device.

v0:
```python
import functools

import jax
import jax.numpy as jnp
from jax import lax
from jax.experimental import pallas as pl
from jax.experimental.pallas import tpu as pltpu
from jax.sharding import PartitionSpec as P

neg_fill = -1000000000.0
epsilon = 1e-06
MESH = pl.DeviceIdType.MESH
f32 = jnp.float32
bf16 = jnp.bfloat16


def dot_nn(a, b):
    return lax.dot_general(a, b, (((1,), (0,)), ((), ())), preferred_element_type=f32)


def dot_nt(a, b):
    return lax.dot_general(a, b, (((1,), (1,)), ((), ())), preferred_element_type=f32)


def dot_tn(a, b):
    return lax.dot_general(a, b, (((0,), (0,)), ((), ())), preferred_element_type=f32)


def relay_kernel(
    sections, n, dps, head_dim,
    stream, cotangent, tokens, buckets, table, gain, wq_hbm, wk_hbm, wv_hbm, wo_hbm,
    grads_out, gain_out, table_out,
    wq, wk, wv, wo, bias, xin, mixg, hp, ip, rad, gin, hs, ins, rads, share, grad,
    raw, proj, probs, inv_kept, acc, mg_ref, sgr, sq, score_kept, tab, gains, ex_h, ex_i,
    w_sem, l_sem, x_s, y_s, x_r, m_s, m_r, h_s, h_r, i_s, i_r, r_s, r_r, g_s, g_r, t_s, t_r, d_s, d_r, fx_s, fm_s, eh_r, ei_r,
):
    micro, seq, width = stream.shape
    heads = bias.shape[0]
    inner = heads * head_dim
    per = 128 // head_dim
    groups = heads // per
    model_width = n * width
    sec = lax.axis_index("section")
    me = lax.axis_index("mp")
    dp = lax.axis_index("dp")
    everyone = sections * dps
    mine = sec * dps + dp
    turn = 1 - 2 * (me // ((n + 1) // 2))

    def peer(i):
        return (me + i * turn + n) % n

    relayed = n == 4
    inner_chip = (me % (n - 1)) != 0 if relayed else True

    def visit(at):
        return jnp.where(at == 1, 2, jnp.where(at == 2, 1, at)) if relayed else at

    def unless_far(i, act):
        if relayed:
            pl.when((i < n - 1) | inner_chip)(act)
        else:
            act()

    def remote(src, dst, ssem, rsem, to_sec, to_mp):
        return pltpu.make_async_remote_copy(
            src_ref=src, dst_ref=dst, send_sem=ssem, recv_sem=rsem,
            device_id={"section": to_sec, "mp": to_mp}, device_id_type=MESH,
        )

    loads = [
        pltpu.make_async_copy(src, dst, w_sem.at[at])
        for at, (src, dst) in enumerate(
            ((wq_hbm.at[0], wq), (wk_hbm.at[0], wk), (wv_hbm.at[0], wv), (wo_hbm.at[0], wo))
        )
    ]
    for load in loads:
        load.start()

    barrier = pltpu.get_barrier_semaphore()
    is_first = sec == 0
    is_last = sec == sections - 1
    for i in range(1, n):
        pl.semaphore_signal(
            barrier, inc=1, device_id={"section": sec, "mp": peer(i)}, device_id_type=MESH
        )

    @pl.when(sec > 0)
    def _():
        for j in range(n):
            pl.semaphore_signal(
                barrier, inc=1, device_id={"section": sec - 1, "mp": j}, device_id_type=MESH
            )

    @pl.when(sec < sections - 1)
    def _():
        for j in range(n):
            pl.semaphore_signal(
                barrier, inc=1, device_id={"section": sec + 1, "mp": j}, device_id_type=MESH
            )

    def member(i):
        return (mine + i) % everyone

    for i in range(1, everyone):
        other = member(i)
        pl.semaphore_signal(
            barrier, inc=1, device_id={"section": other // dps, "dp": other % dps},
            device_id_type=MESH,
        )

    greeters = n - 1 + everyone - 1 + n * jnp.minimum(sec, 1) + n * jnp.minimum(sections - 1 - sec, 1)
    pl.semaphore_wait(barrier, greeters)

    def x_copy(m, j):
        return remote(stream.at[m], xin.at[m, me], x_s.at[m, j], x_r.at[m, me], sec, j)

    def y_copy(m, j):
        return remote(share.at[m], xin.at[m, me], y_s.at[m, j], x_r.at[m, me], sec + 1, j)

    @pl.when(is_first)
    def _():
        for m in range(micro):
            pltpu.make_async_copy(stream.at[m], xin.at[m, me], l_sem.at[m]).start()
            for i in range(n - 1, 0, -1):
                unless_far(i, lambda m=m, i=i: x_copy(m, peer(i)).start())

    def head_bias(h, carry):
        value = jnp.zeros((seq, seq), f32)
        held = buckets[...]
        for c in range(table.shape[1]):
            value = jnp.where(held == c, table[h, c], value)
        bias[h] = value
        return carry

    lax.fori_loop(0, heads, head_bias, 0)
    tab[mine] = jnp.zeros(tab.shape[1:], f32)
    gains[dp] = jnp.zeros(gains.shape[1:], f32)
    for load in loads:
        load.wait()

    def h_copy(m, j):
        return remote(hs.at[m, j], hp.at[m, me], h_s.at[m, j], h_r.at[m, me], sec, j)

    def emit(at):
        return jnp.where(at == 0, 3, jnp.where(at == 3, 2, 2 - at)) if relayed else n - 1 - at

    def pass_on(m, i, part, own, extra, own_sem, extra_sem, copy):
        j = peer(i)
        own[m, j] = part.astype(bf16)
        if not relayed:
            pl.when(i > 0)(lambda: copy(m, j).start())
            return

        def hand_over():
            return remote(own.at[m, j], extra.at[m], own_sem.at[m, j], extra_sem.at[m], sec, peer(1))

        @pl.when((i == n - 2) & inner_chip)
        def _():
            hand_over().wait_recv()
            own[m, j] = (part + extra[m].astype(f32)).astype(bf16)

        @pl.when((i > 0) & ((i < n - 1) | inner_chip))
        def _():
            copy(m, j).start()

        @pl.when((i == n - 1) & ((me % (n - 1)) == 0))
        def _():
            hand_over().start()

    def head_parts(m, upstream):
        def one(step, carry):
            i = emit(step)
            j = peer(i)
            rows = wo[pl.ds(pl.multiple_of(j * inner, inner), inner), :]
            pass_on(m, i, dot_nt(upstream[m], rows), hs, ex_h, h_s, eh_r, h_copy)

            return carry

        lax.fori_loop(0, n, one, 0)

    @pl.when(is_last)
    def _():
        def one(m, carry):
            head_parts(m, cotangent)
            return carry

        lax.fori_loop(0, micro, one, 0)

    lane = lax.broadcasted_iota(jnp.int32, (1, 128), 1)
    picks = [
        jnp.where((lane // head_dim) == e, 1.0, 0.0).astype(f32) for e in range(per)
    ]
    picks_half = [pick.astype(bf16) for pick in picks]

    def spread(block):
        return jnp.concatenate([block * pick for pick in picks_half], axis=0)

    def fold(block):
        total = block[:seq] * picks[0]
        for e in range(1, per):
            total = total + block[e * seq : (e + 1) * seq] * picks[e]
        return total

    def mix_copy(m, j):
        return remote(mixg.at[m, me], mixg.at[m, me], m_s.at[m, j], m_r.at[m, me], sec, j)

    def on_x(m, j):
        return remote(xin.at[m, j], xin.at[m, j], fx_s.at[m], x_r.at[m, j], sec, peer(n - 1))

    def on_mix(m, j):
        return remote(mixg.at[m, j], mixg.at[m, j], fm_s.at[m], m_r.at[m, j], sec, peer(n - 1))

    def forward(m):
        @pl.when(is_first)
        def _():
            pltpu.make_async_copy(stream.at[m], xin.at[m, me], l_sem.at[m]).wait()

        raw[m] = jnp.zeros(raw.shape[1:], f32)
        sq[...] = jnp.zeros(sq.shape, f32)

        def gathered(at, inside):
            i = visit(at)
            j = peer(i)

            @pl.when((sec > 0) | (i > 0))
            def _():
                remote(
                    share.at[m], xin.at[m, j], x_s.at[m, j], x_r.at[m, j], sec, j
                ).wait_recv()

            if relayed:

                @pl.when((i == n - 2) & inner_chip)
                def _():
                    on_x(m, j).start()

            piece = xin[m, j].astype(f32)
            sq[...] += jnp.sum(piece * piece, axis=1, keepdims=True)
            cols = pl.ds(pl.multiple_of(j * width, width), width)
            scaled = (piece * gain[:, cols]).astype(bf16)
            rows = pl.ds(pl.multiple_of(j * width, width), width)
            for at, w in enumerate((wq, wk, wv)):
                raw[m, :, at * inner : (at + 1) * inner] += dot_nn(scaled, w[rows, :])
            return inside

        lax.fori_loop(0, n, gathered, 0)
        inv = lax.rsqrt(sq[:, :1] / model_width + epsilon)
        inv_kept[m] = jnp.broadcast_to(inv, (seq, 128))
        proj[m] = (raw[m] * inv).astype(bf16)
        mask_row = jnp.where(tokens[pl.ds(m, 1), :] == 0, neg_fill, 0.0)
        for p in range(groups):
            cols = slice(p * 128, (p + 1) * 128)
            q = proj[m, :, p * 128 : (p + 1) * 128]
            k = proj[m, :, inner + p * 128 : inner + (p + 1) * 128]
            v = proj[m, :, 2 * inner + p * 128 : 2 * inner + (p + 1) * 128]
            scores = dot_nt(spread(q), k)
            scores = scores + bias[p * per : (p + 1) * per].reshape(per * seq, seq) + mask_row
            top = jnp.max(scores, axis=-1, keepdims=True)
            grown = jnp.exp(scores - top)
            prob = grown / jnp.sum(grown, axis=-1, keepdims=True)
            probs[m, p] = prob
            mixg[m, me, :, cols] = fold(dot_nn(prob.astype(bf16), v)).astype(bf16)

        @pl.when(sec < sections - 1)
        def _():
            for i in range(n - 1, 0, -1):
                unless_far(i, lambda i=i: mix_copy(m, peer(i)).start())

    def project(m):
        @pl.when(sec < sections - 1)
        def _():
            acc[...] = xin[m, me].astype(f32)

            def mixed(at, inside):
                i = visit(at)
                j = peer(i)

                @pl.when(i > 0)
                def _():
                    remote(
                        mixg.at[m, j], mixg.at[m, j], m_s.at[m, j], m_r.at[m, j], sec, j
                    ).wait_recv()

                if relayed:

                    @pl.when((i == n - 2) & inner_chip)
                    def _():
                        on_mix(m, j).start()

                rows = pl.ds(pl.multiple_of(j * inner, inner), inner)
                acc[...] += dot_nn(mixg[m, j], wo[rows, :])
                return inside

            lax.fori_loop(0, n, mixed, 0)
            share[m] = acc[...].astype(bf16)
            for i in range(n - 1, -1, -1):
                unless_far(i, lambda i=i: y_copy(m, peer(i)).start())

    def i_copy(m, j):
        return remote(ins.at[m, j], ip.at[m, me], i_s.at[m, j], i_r.at[m, me], sec, j)

    def r_copy(m, j):
        return remote(rads.at[m], rad.at[m, me], r_s.at[m, j], r_r.at[m, me], sec, j)

    def g_copy(m, to_sec):
        return remote(grad.at[m], gin.at[m], g_s.at[m], g_r.at[m], to_sec, me)

    def t_copy(i):
        other = member(i)
        return pltpu.make_async_remote_copy(
            src_ref=tab.at[mine], dst_ref=tab.at[mine],
            send_sem=t_s.at[other], recv_sem=t_r.at[mine],
            device_id={"section": other // dps, "dp": other % dps}, device_id_type=MESH,
        )

    def d_copy(i):
        other = (dp + i) % dps
        return pltpu.make_async_remote_copy(
            src_ref=gains.at[dp], dst_ref=gains.at[dp],
            send_sem=d_s.at[other], recv_sem=d_r.at[dp],
            device_id={"dp": other}, device_id_type=MESH,
        )

    def backward(m):
        @pl.when(is_last)
        def _():
            gin[m] = cotangent[m]

        @pl.when(sec < sections - 1)
        def _():
            g_copy(m, sec + 1).wait_recv()
            head_parts(m, gin)

        mg_ref[...] = hs[m, me].astype(f32)

        def arrived(i, inside):
            j = peer(i)

            def add():
                remote(hs.at[m, j], hp.at[m, j], h_s.at[m, j], h_r.at[m, j], sec, j).wait_recv()
                mg_ref[...] += hp[m, j].astype(f32)

            unless_far(i, add)
            return inside

        lax.fori_loop(1, n, arrived, 0)
        inv = inv_kept[m][:, :1]
        radial = jnp.zeros((seq, 128), f32)
        for p in range(groups):
            q_cols = slice(p * 128, (p + 1) * 128)
            k_cols = slice(inner + p * 128, inner + (p + 1) * 128)
            v_cols = slice(2 * inner + p * 128, 2 * inner + (p + 1) * 128)
            q2 = spread(proj[m, :, q_cols])
            k = proj[m, :, k_cols]
            v = proj[m, :, v_cols]
            mg2 = spread(mg_ref[:, q_cols].astype(bf16))
            prob = probs[m, p]
            prob_grad = dot_nt(mg2, v)
            value_grad = dot_tn(prob.astype(bf16), mg2)
            score_grad = prob * (prob_grad - jnp.sum(prob_grad * prob, axis=-1, keepdims=True))
            score_kept[p * per : (p + 1) * per] = score_grad.reshape(per, seq, seq)
            half = score_grad.astype(bf16)
            query_grad = fold(dot_nn(half, k))
            key_grad = dot_tn(half, q2)
            for cols, part in ((q_cols, query_grad), (k_cols, key_grad), (v_cols, value_grad)):
                radial = radial + part * raw[m, :, cols]
                sgr[:, cols] = (part * inv).astype(bf16)
        rads[m] = jnp.broadcast_to(jnp.sum(radial, axis=1, keepdims=True), (seq, 128)).T[:8]
        for i in range(n - 1, 0, -1):
            r_copy(m, peer(i)).start()

        def input_part(step, inside):
            i = emit(step)
            j = peer(i)
            rows = pl.ds(pl.multiple_of(j * width, width), width)
            part = dot_nt(sgr[:, :inner], wq[rows, :])
            part += dot_nt(sgr[:, inner : 2 * inner], wk[rows, :])
            part += dot_nt(sgr[:, 2 * inner :], wv[rows, :])
            pass_on(m, i, part, ins, ex_i, i_s, ei_r, i_copy)
            return inside

        lax.fori_loop(0, n, input_part, 0)

        def bucket_part(c, inside):
            picked = jnp.where((buckets[...] == c)[None], score_kept[...], 0.0)
            part = jnp.sum(jnp.sum(picked, axis=1), axis=1, keepdims=True)
            tab[mine, :heads] += jnp.where(lane == c, part, 0.0)
            return inside

        lax.fori_loop(0, table.shape[1], bucket_part, 0)

        @pl.when(m == micro - 1)
        def _():
            for i in range(1, everyone):
                t_copy(i).start()

        acc[...] = ins[m, me].astype(f32)
        sq[:8, :seq] = rads[m]

        def arrived_input(i, inside):
            j = peer(i)
            remote(rads.at[m], rad.at[m, j], r_s.at[m, j], r_r.at[m, j], sec, j).wait_recv()
            sq[:8, :seq] += rad[m, j]

            def add():
                remote(ins.at[m, j], ip.at[m, j], i_s.at[m, j], i_r.at[m, j], sec, j).wait_recv()
                acc[...] += ip[m, j].astype(f32)

            unless_far(i, add)
            return inside

        lax.fori_loop(1, n, arrived_input, 0)
        radial_sum = jnp.broadcast_to(sq[:1, :seq], (128, seq)).T[:, :1]
        rows_f32 = xin[m, me].astype(f32)
        normed = acc[...]
        gain_own = gain[:, pl.ds(pl.multiple_of(me * width, width), width)]
        weight = radial_sum * inv * inv * inv / model_width
        result = (gin[m].astype(f32) + normed * gain_own - weight * rows_f32).astype(bf16)
        grad[m] = result
        grads_out[0, m] = result

        @pl.when(sec > 0)
        def _():
            g_copy(m, sec - 1).start()

        gains[dp] += jnp.sum(normed * rows_f32, axis=0, keepdims=True)

    def step(t, carry):
        early = t < 2 * micro
        kind = jnp.where(early, jnp.where(is_first, t // micro, t % 2), 2)
        m = jnp.where(early, jnp.where(is_first, t % micro, t // 2), t - 2 * micro)
        kind = jnp.where(is_last, t % 3, kind)
        m = jnp.where(is_last, t // 3, m)

        @pl.when(kind == 0)
        def _():
            forward(m)

        @pl.when(kind == 1)
        def _():
            project(m)

        @pl.when(kind == 2)
        def _():
            backward(m)

        return carry

    lax.fori_loop(0, 3 * micro, step, 0)
    for i in range(1, dps):
        d_copy(i).start()

    def finish(m, carry):
        def one(i, inside):
            j = peer(i)
            h_copy(m, j).wait_send()
            i_copy(m, j).wait_send()
            r_copy(m, j).wait_send()

            @pl.when(is_first)
            def _():
                unless_far(i, lambda: x_copy(m, j).wait_send())

            @pl.when(sec < sections - 1)
            def _():
                unless_far(i, lambda: mix_copy(m, j).wait_send())

            return inside

        lax.fori_loop(1, n, one, 0)
        if relayed:

            @pl.when(inner_chip)
            def _():
                on_x(m, peer(n - 2)).wait_send()

            @pl.when(inner_chip & (sec < sections - 1))
            def _():
                on_mix(m, peer(n - 2)).wait_send()

        @pl.when(sec > 0)
        def _():
            g_copy(m, sec - 1).wait_send()

        return carry

    lax.fori_loop(0, micro, finish, 0)

    @pl.when(sec < sections - 1)
    def _():
        def one(m, carry):
            for i in range(n):
                unless_far(i, lambda i=i: y_copy(m, peer(i)).wait_send())
            return carry

        lax.fori_loop(0, micro, one, 0)

    def table_wait(i, carry):
        other = member(i)
        pltpu.make_async_remote_copy(
            src_ref=tab.at[mine], dst_ref=tab.at[other],
            send_sem=t_s.at[other], recv_sem=t_r.at[other],
            device_id={"section": other // dps, "dp": other % dps}, device_id_type=MESH,
        ).wait()
        return carry

    lax.fori_loop(1, everyone, table_wait, 0)
    total = tab[0]
    for at in range(1, everyone):
        total = total + tab[at]
    table_out[...] = total[:heads, : table_out.shape[1]]
    for i in range(1, dps):
        other = (dp + i) % dps
        pltpu.make_async_remote_copy(
            src_ref=gains.at[dp], dst_ref=gains.at[other],
            send_sem=d_s.at[other], recv_sem=d_r.at[other],
            device_id={"dp": other}, device_id_type=MESH,
        ).wait()
    total = gains[0]
    for at in range(1, dps):
        total = total + gains[at]
    gain_out[...] = total


def per_device(
    stream, cotangent, token_ids, buckets, bias_table, gain, w_query, w_key, w_value, w_out
):
    sections = lax.axis_size("section")
    n = lax.axis_size("mp")
    dps = lax.axis_size("dp")
    micro, seq, width = stream.shape
    heads = bias_table.shape[1]
    inner = w_query.shape[2]
    head_dim = inner // heads
    groups = heads * head_dim // 128
    per = 128 // head_dim
    vmem = pl.BlockSpec(memory_space=pltpu.VMEM)
    hbm = pl.BlockSpec(memory_space=pl.ANY)
    dma = pltpu.SemaphoreType.DMA
    grads, gains, table_grad = pl.pallas_call(
        functools.partial(relay_kernel, sections, n, dps, head_dim),
        out_shape=(
            jax.ShapeDtypeStruct((1, micro, seq, width), bf16),
            jax.ShapeDtypeStruct((1, width), f32),
            jax.ShapeDtypeStruct(bias_table.shape[::-1], f32),
        ),
        in_specs=[vmem, vmem, vmem, vmem, pl.BlockSpec(memory_space=pltpu.SMEM), vmem]
        + [hbm] * 4,
        out_specs=(vmem, vmem, vmem),
        scratch_shapes=[
            pltpu.VMEM(w_query.shape[1:], bf16),
            pltpu.VMEM(w_key.shape[1:], bf16),
            pltpu.VMEM(w_value.shape[1:], bf16),
            pltpu.VMEM(w_out.shape[1:], bf16),
            pltpu.VMEM((heads, seq, seq), f32),
            pltpu.VMEM((micro, n, seq, width), bf16),
            pltpu.VMEM((micro, n, seq, inner), bf16),
            pltpu.VMEM((micro, n, seq, inner), bf16),
            pltpu.VMEM((micro, n, seq, width), bf16),
            pltpu.VMEM((micro, n, 8, seq), f32),
            pltpu.VMEM((micro, seq, width), bf16),
            pltpu.VMEM((micro, n, seq, inner), bf16),
            pltpu.VMEM((micro, n, seq, width), bf16),
            pltpu.VMEM((micro, 8, seq), f32),
            pltpu.VMEM((micro, seq, width), bf16),
            pltpu.VMEM((micro, seq, width), bf16),
            pltpu.VMEM((micro, seq, 3 * inner), f32),
            pltpu.VMEM((micro, seq, 3 * inner), bf16),
            pltpu.VMEM((micro, groups, per * seq, seq), f32),
            pltpu.VMEM((micro, seq, 128), f32),
            pltpu.VMEM((seq, width), f32),
            pltpu.VMEM((seq, inner), f32),
            pltpu.VMEM((seq, 3 * inner), bf16),
            pltpu.VMEM((seq, 128), f32),
            pltpu.VMEM((heads, seq, seq), f32),
            pltpu.VMEM((sections * dps, max(heads, 8), 128), f32),
            pltpu.VMEM((dps, 1, width), f32),
            pltpu.VMEM((micro, seq, inner), bf16),
            pltpu.VMEM((micro, seq, width), bf16),
            dma((4,)),
            dma((micro,)),
        ]
        + [dma((micro, n))] * 11
        + [dma((micro,))] * 2
        + [dma((sections * dps,))] * 2
        + [dma((dps,))] * 2
        + [dma((micro,))] * 4,
        compiler_params=pltpu.CompilerParams(
            collective_id=0, has_side_effects=True, vmem_limit_bytes=60 * 1024 * 1024
        ),
    )(
        stream, cotangent, token_ids, buckets, bias_table.T, gain, w_query, w_key, w_value, w_out,
    )
    return grads, gains, table_grad.T


def solution(mesh):
    in_specs = (
        P("dp", None, "mp"),
        P("dp", None, "mp"),
        P("dp", None),
        P(),
        P(None, "mp"),
        P("section", None),
        P("section", None, "mp"),
        P("section", None, "mp"),
        P("section", None, "mp"),
        P("section", None, "mp"),
    )
    out_specs = (P("section", "dp", None, "mp"), P("section", "mp"), P(None, "mp"))
    return jax.shard_map(
        per_device, mesh=mesh, in_specs=in_specs, out_specs=out_specs, check_vma=False
    )
```

profile of v0, /device:TPU:0, one launch (start us, length us, event | category | flops | bytes accessed | tf_op | source)
XLA Modules:
  0.0 212.5 jit_solution(12118282254881281898)
XLA Ops:
  0.6 207.6 %shard_map.121 = (bf16[1,2,64,1024]{3,2,1,0:T(8,128)(2,1)}, f32[1,1024]{1,0:T(1,128)}, f32[8,32]{1,0:T(8,128)}) custom-call(bf16[2,64,1024]{2,1,0:T(8,128)(2,1)} %stream.1, bf16[2,64,1024]{2,1,0:T(8,128)(2,1)} %cotangent.1, s32[2,64]{1,0:T(2,128)} %tokens.1, s32[64,64]{1,0:T(8,128)} %buckets.1, f32[8,32]{1,0:T(8,128)} %bitcast.3, f32[1,4096]{1,0:T(1,128)} %gain.1, ...), custom_call_target="tpu_custom_call" | custom-call | tf_op jit(solution)/shard_map/pallas_call | solution.py:541
  208.2 1.7 copy.16
  209.9 1.3 copy.17
  211.2 1.3 copy.18
where the time goes:
time: 213 us; the launch traced here: 212 us
  Pallas kernels  208 us (98%)
  local copies, waits for them, and re-layouts  4.22 us (2%)
    pallas_call x1, Pallas kernels, per_device(): pl.pallas_call(functools.partial(relay_kernel, sections, n, dps, head_dim...  208 us

commit v1 on v0

--- a/solution.py
+++ b/solution.py
@@ -10,6 +10,8 @@
 neg_fill = -1000000000.0
 epsilon = 1e-06
 MESH = pl.DeviceIdType.MESH
+DELAY = 8000
+DELAYED = 1
 f32 = jnp.float32
 bf16 = jnp.bfloat16
 
@@ -31,7 +33,7 @@
     stream, cotangent, tokens, buckets, table, gain, wq_hbm, wk_hbm, wv_hbm, wo_hbm,
     grads_out, gain_out, table_out,
     wq, wk, wv, wo, bias, xin, mixg, hp, ip, rad, gin, hs, ins, rads, share, grad,
-    raw, proj, probs, inv_kept, acc, mg_ref, sgr, sq, score_kept, tab, gains, ex_h, ex_i,
+    raw, proj, probs, inv_kept, acc, mg_ref, sgr, sq, diag, tab, gains, ex_h, ex_i,
     w_sem, l_sem, x_s, y_s, x_r, m_s, m_r, h_s, h_r, i_s, i_r, r_s, r_r, g_s, g_r, t_s, t_r, d_s, d_r, fx_s, fm_s, eh_r, ei_r,
 ):
     micro, seq, width = stream.shape
@@ -118,12 +120,18 @@
     def y_copy(m, j):
         return remote(share.at[m], xin.at[m, me], y_s.at[m, j], x_r.at[m, me], sec + 1, j)
 
+    def send_x(m):
+        pltpu.make_async_copy(stream.at[m], xin.at[m, me], l_sem.at[m]).start()
+        for i in range(n - 1, 0, -1):
+            unless_far(i, lambda i=i: x_copy(m, peer(i)).start())
+
     @pl.when(is_first)
     def _():
-        for m in range(micro):
-            pltpu.make_async_copy(stream.at[m], xin.at[m, me], l_sem.at[m]).start()
-            for i in range(n - 1, 0, -1):
-                unless_far(i, lambda m=m, i=i: x_copy(m, peer(i)).start())
+        @pl.when(dp % 2 == DELAYED)
+        def _():
+            pl.delay(DELAY)
+
+        send_x(0)
 
     def head_bias(h, carry):
         value = jnp.zeros((seq, seq), f32)
@@ -135,6 +143,7 @@
 
     lax.fori_loop(0, heads, head_bias, 0)
     tab[mine] = jnp.zeros(tab.shape[1:], f32)
+    diag[...] = jnp.zeros(diag.shape, f32)
     gains[dp] = jnp.zeros(gains.shape[1:], f32)
     for load in loads:
         load.wait()
@@ -267,6 +276,10 @@
             for i in range(n - 1, 0, -1):
                 unless_far(i, lambda i=i: mix_copy(m, peer(i)).start())
 
+        @pl.when(is_first & (m + 1 < micro))
+        def _():
+            send_x(m + 1)
+
     def project(m):
         @pl.when(sec < sections - 1)
         def _():
@@ -322,15 +335,14 @@
             device_id={"dp": other}, device_id_type=MESH,
         )
 
+    def receive(m):
+        g_copy(m, sec + 1).wait_recv()
+        head_parts(m, gin)
+
     def backward(m):
         @pl.when(is_last)
         def _():
             gin[m] = cotangent[m]
-
-        @pl.when(sec < sections - 1)
-        def _():
-            g_copy(m, sec + 1).wait_recv()
-            head_parts(m, gin)
 
         mg_ref[...] = hs[m, me].astype(f32)
 
@@ -359,7 +371,14 @@
             prob_grad = dot_nt(mg2, v)
             value_grad = dot_tn(prob.astype(bf16), mg2)
             score_grad = prob * (prob_grad - jnp.sum(prob_grad * prob, axis=-1, keepdims=True))
-            score_kept[p * per : (p + 1) * per] = score_grad.reshape(per, seq, seq)
+            wide = jnp.concatenate([score_grad, jnp.zeros_like(score_grad)], axis=1)
+            for e in range(per):
+                part = wide[e * seq : e * seq + 8]
+                for a in range(8, seq, 8):
+                    part = part + pltpu.roll(
+                        wide[e * seq + a : e * seq + a + 8], (2 * seq - a) % (2 * seq), 1
+                    )
+                diag[p * per + e] += part
             half = score_grad.astype(bf16)
             query_grad = fold(dot_nn(half, k))
             key_grad = dot_tn(half, q2)
@@ -382,19 +401,20 @@
 
         lax.fori_loop(0, n, input_part, 0)
 
-        def bucket_part(c, inside):
-            picked = jnp.where((buckets[...] == c)[None], score_kept[...], 0.0)
-            part = jnp.sum(jnp.sum(picked, axis=1), axis=1, keepdims=True)
-            tab[mine, :heads] += jnp.where(lane == c, part, 0.0)
-            return inside
-
-        lax.fori_loop(0, table.shape[1], bucket_part, 0)
-
         @pl.when(m == micro - 1)
         def _():
+            sub = lax.broadcasted_iota(jnp.int32, (8, 2 * seq), 0)
+            for h in range(heads):
+                part = diag[h]
+                for bit in (1, 2, 4):
+                    moved = pltpu.roll(part, 2 * seq - bit, 1)
+                    part = jnp.where((sub // bit) % 2 == 1, moved, part)
+                tab[mine, h : h + 1] = jnp.sum(part, axis=0, keepdims=True)
             for i in range(1, everyone):
                 t_copy(i).start()
 
+    def settle(m):
+        inv = inv_kept[m][:, :1]
         acc[...] = ins[m, me].astype(f32)
         sq[:8, :seq] = rads[m]
 
@@ -427,27 +447,20 @@
         gains[dp] += jnp.sum(normed * rows_f32, axis=0, keepdims=True)
 
     def step(t, carry):
-        early = t < 2 * micro
-        kind = jnp.where(early, jnp.where(is_first, t // micro, t % 2), 2)
-        m = jnp.where(early, jnp.where(is_first, t % micro, t // 2), t - 2 * micro)
-        kind = jnp.where(is_last, t % 3, kind)
+        u = t - 2 * micro
+        kind = jnp.where(u < 0, t % 2, u % 3 + 2)
+        m = jnp.where(u < 0, t // 2, u // 3)
+        of_last = t % 3
+        kind = jnp.where(is_last, jnp.where(of_last == 0, 0, of_last + 2), kind)
         m = jnp.where(is_last, t // 3, m)
-
-        @pl.when(kind == 0)
-        def _():
-            forward(m)
-
-        @pl.when(kind == 1)
-        def _():
-            project(m)
-
-        @pl.when(kind == 2)
-        def _():
-            backward(m)
+        busy = ~is_last | (t < 3 * micro)
+
+        for at, act in enumerate((forward, project, receive, backward, settle)):
+            pl.when((kind == at) & busy)(lambda act=act: act(m))
 
         return carry
 
-    lax.fori_loop(0, 3 * micro, step, 0)
+    lax.fori_loop(0, 5 * micro, step, 0)
     for i in range(1, dps):
         d_copy(i).start()
 
@@ -509,7 +522,13 @@
     total = tab[0]
     for at in range(1, everyone):
         total = total + tab[at]
-    table_out[...] = total[:heads, : table_out.shape[1]]
+    last = buckets[seq - 1 : seq, :]
+    place = jnp.concatenate([buckets[0:1, :], last[:, seq - 1 :], last[:, : seq - 1]], axis=1)
+    summed = jnp.zeros(total.shape, f32)
+    for c in range(table.shape[1]):
+        part = jnp.sum(jnp.where(place == c, total, 0.0), axis=1, keepdims=True)
+        summed = jnp.where(lane == c, part, summed)
+    table_out[...] = summed[:heads, : table_out.shape[1]]
     for i in range(1, dps):
         other = (dp + i) % dps
         pltpu.make_async_remote_copy(
@@ -573,8 +592,8 @@
             pltpu.VMEM((seq, inner), f32),
             pltpu.VMEM((seq, 3 * inner), bf16),
             pltpu.VMEM((seq, 128), f32),
-            pltpu.VMEM((heads, seq, seq), f32),
-            pltpu.VMEM((sections * dps, max(heads, 8), 128), f32),
+            pltpu.VMEM((heads, 8, 2 * seq), f32),
+            pltpu.VMEM((sections * dps, max(heads, 8), 2 * seq), f32),
             pltpu.VMEM((dps, 1, width), f32),
             pltpu.VMEM((micro, seq, inner), bf16),
             pltpu.VMEM((micro, seq, width), bf16),

time: 213 us -> 197 us (0.925)
  Pallas kernels: 208 us -> 191 us
    pallas_call x1, Pallas kernels: 208 us -> 191 us  [per_device(): pl.pallas_call(functools.partial(relay_kernel, sections, n, dps, head_dim...]
where the time goes in v1:
time: 197 us; the launch traced here: 196 us
  Pallas kernels  191 us (97%)
  local copies, waits for them, and re-layouts  4.22 us (2%)
    pallas_call x1, Pallas kernels, per_device(): pl.pallas_call(functools.partial(relay_kernel, sections, n, dps, head_dim...  191 us
    unnamed x3, local copies, waits for them, and re-layouts  4.22 us

profile of v1, /device:TPU:0, one launch (start us, length us, event | category | flops | bytes accessed | tf_op | source)
XLA Modules:
  0.0 196.3 jit_solution(4233633413477104601)
XLA Ops:
  0.6 191.4 %shard_map.121 = (bf16[1,2,64,1024]{3,2,1,0:T(8,128)(2,1)}, f32[1,1024]{1,0:T(1,128)}, f32[8,32]{1,0:T(8,128)}) custom-call(bf16[2,64,1024]{2,1,0:T(8,128)(2,1)} %stream.1, bf16[2,64,1024]{2,1,0:T(8,128)(2,1)} %cotangent.1, s32[2,64]{1,0:T(2,128)} %tokens.1, s32[64,64]{1,0:T(8,128)} %buckets.1, f32[8,32]{1,0:T(8,128)} %bitcast.3, f32[1,4096]{1,0:T(1,128)} %gain.1, ...), custom_call_target="tpu_custom_call" | custom-call | tf_op jit(solution)/shard_map/pallas_call | solution.py:560
  192.1 1.7 copy.16
  193.7 1.3 copy.17
  195.0 1.3 copy.18

commit v2 on v1

--- a/solution.py
+++ b/solution.py
@@ -32,7 +32,7 @@
     sections, n, dps, head_dim,
     stream, cotangent, tokens, buckets, table, gain, wq_hbm, wk_hbm, wv_hbm, wo_hbm,
     grads_out, gain_out, table_out,
-    wq, wk, wv, wo, bias, xin, mixg, hp, ip, rad, gin, hs, ins, rads, share, grad,
+    wq, wk, wv, wo, wq_t, wk_t, wv_t, wo_t, bias, xin, mixg, hp, ip, rad, gin, hs, ins, rads, share, grad,
     raw, proj, probs, inv_kept, acc, mg_ref, sgr, sq, diag, tab, gains, ex_h, ex_i,
     w_sem, l_sem, x_s, y_s, x_r, m_s, m_r, h_s, h_r, i_s, i_r, r_s, r_r, g_s, g_r, t_s, t_r, d_s, d_r, fx_s, fm_s, eh_r, ei_r,
 ):
@@ -53,6 +53,30 @@
         return (me + i * turn + n) % n
 
     relayed = n == 4
+    chunks = 2 if relayed and inner % 256 == 0 and width % 256 == 0 else 1
+    in_half, mix_half = width // chunks, inner // chunks
+
+    def in_cols(c):
+        return pl.ds(pl.multiple_of(c * in_half, in_half), in_half)
+
+    def mix_cols(c):
+        return pl.ds(pl.multiple_of(c * mix_half, mix_half), mix_half)
+
+    def flip(src, dst):
+        rows = min(256, src.shape[0])
+
+        def one(r, carry):
+            at = pl.ds(pl.multiple_of(r * rows, rows), rows)
+            dst[:, at] = src[at, :].T
+            return carry
+
+        lax.fori_loop(0, src.shape[0] // rows, one, 0)
+
+    def flip_all():
+        for src, dst in ((wo, wo_t), (wq, wq_t), (wk, wk_t), (wv, wv_t)):
+            flip(src, dst)
+
+    flips_first = sec * 2 >= sections
     inner_chip = (me % (n - 1)) != 0 if relayed else True
 
     def visit(at):
@@ -114,16 +138,23 @@
     greeters = n - 1 + everyone - 1 + n * jnp.minimum(sec, 1) + n * jnp.minimum(sections - 1 - sec, 1)
     pl.semaphore_wait(barrier, greeters)
 
-    def x_copy(m, j):
-        return remote(stream.at[m], xin.at[m, me], x_s.at[m, j], x_r.at[m, me], sec, j)
-
-    def y_copy(m, j):
-        return remote(share.at[m], xin.at[m, me], y_s.at[m, j], x_r.at[m, me], sec + 1, j)
+    def x_copy(m, j, c):
+        return remote(
+            stream.at[m, :, in_cols(c)], xin.at[m, me, :, in_cols(c)],
+            x_s.at[m, j, c], x_r.at[m, me, c], sec, j,
+        )
+
+    def y_copy(m, j, c):
+        return remote(
+            share.at[m, :, in_cols(c)], xin.at[m, me, :, in_cols(c)],
+            y_s.at[m, j, c], x_r.at[m, me, c], sec + 1, j,
+        )
 
     def send_x(m):
         pltpu.make_async_copy(stream.at[m], xin.at[m, me], l_sem.at[m]).start()
-        for i in range(n - 1, 0, -1):
-            unless_far(i, lambda i=i: x_copy(m, peer(i)).start())
+        for c in range(chunks):
+            for i in range(n - 1, 0, -1):
+                unless_far(i, lambda i=i, c=c: x_copy(m, peer(i), c).start())
 
     @pl.when(is_first)
     def _():
@@ -147,31 +178,38 @@
     gains[dp] = jnp.zeros(gains.shape[1:], f32)
     for load in loads:
         load.wait()
-
-    def h_copy(m, j):
-        return remote(hs.at[m, j], hp.at[m, me], h_s.at[m, j], h_r.at[m, me], sec, j)
+    pl.when(flips_first)(flip_all)
+
+    def h_copy(m, j, c):
+        return remote(
+            hs.at[m, j, :, mix_cols(c)], hp.at[m, me, :, mix_cols(c)],
+            h_s.at[m, j, c], h_r.at[m, me, c], sec, j,
+        )
 
     def emit(at):
         return jnp.where(at == 0, 3, jnp.where(at == 3, 2, 2 - at)) if relayed else n - 1 - at
 
-    def pass_on(m, i, part, own, extra, own_sem, extra_sem, copy):
+    def pass_on(m, i, c, cols, part, own, extra, own_sem, extra_sem, copy):
         j = peer(i)
-        own[m, j] = part.astype(bf16)
+        own[m, j, :, cols] = part.astype(bf16)
         if not relayed:
-            pl.when(i > 0)(lambda: copy(m, j).start())
+            pl.when(i > 0)(lambda: copy(m, j, c).start())
             return
 
         def hand_over():
-            return remote(own.at[m, j], extra.at[m], own_sem.at[m, j], extra_sem.at[m], sec, peer(1))
+            return remote(
+                own.at[m, j, :, cols], extra.at[m, :, cols],
+                own_sem.at[m, j, c], extra_sem.at[m, c], sec, peer(1),
+            )
 
         @pl.when((i == n - 2) & inner_chip)
         def _():
             hand_over().wait_recv()
-            own[m, j] = (part + extra[m].astype(f32)).astype(bf16)
+            own[m, j, :, cols] = (part + extra[m, :, cols].astype(f32)).astype(bf16)
 
         @pl.when((i > 0) & ((i < n - 1) | inner_chip))
         def _():
-            copy(m, j).start()
+            copy(m, j, c).start()
 
         @pl.when((i == n - 1) & ((me % (n - 1)) == 0))
         def _():
@@ -181,9 +219,11 @@
         def one(step, carry):
             i = emit(step)
             j = peer(i)
-            rows = wo[pl.ds(pl.multiple_of(j * inner, inner), inner), :]
-            pass_on(m, i, dot_nt(upstream[m], rows), hs, ex_h, h_s, eh_r, h_copy)
-
+            cols = pl.ds(pl.multiple_of(j * inner, inner), inner)
+            part = dot_nn(upstream[m], wo_t[:, cols])
+            for c in range(chunks):
+                at = slice(c * mix_half, (c + 1) * mix_half)
+                pass_on(m, i, c, at, part[:, at], hs, ex_h, h_s, eh_r, h_copy)
             return carry
 
         lax.fori_loop(0, n, one, 0)
@@ -211,14 +251,17 @@
             total = total + block[e * seq : (e + 1) * seq] * picks[e]
         return total
 
-    def mix_copy(m, j):
-        return remote(mixg.at[m, me], mixg.at[m, me], m_s.at[m, j], m_r.at[m, me], sec, j)
-
-    def on_x(m, j):
-        return remote(xin.at[m, j], xin.at[m, j], fx_s.at[m], x_r.at[m, j], sec, peer(n - 1))
-
-    def on_mix(m, j):
-        return remote(mixg.at[m, j], mixg.at[m, j], fm_s.at[m], m_r.at[m, j], sec, peer(n - 1))
+    def mix_copy(m, j, c):
+        part = mixg.at[m, me, :, mix_cols(c)]
+        return remote(part, part, m_s.at[m, j, c], m_r.at[m, me, c], sec, j)
+
+    def on_x(m, j, c):
+        part = xin.at[m, j, :, in_cols(c)]
+        return remote(part, part, fx_s.at[m, c], x_r.at[m, j, c], sec, peer(n - 1))
+
+    def on_mix(m, j, c):
+        part = mixg.at[m, j, :, mix_cols(c)]
+        return remote(part, part, fm_s.at[m, c], m_r.at[m, j, c], sec, peer(n - 1))
 
     def forward(m):
         @pl.when(is_first)
@@ -228,32 +271,33 @@
         raw[m] = jnp.zeros(raw.shape[1:], f32)
         sq[...] = jnp.zeros(sq.shape, f32)
 
-        def gathered(at, inside):
-            i = visit(at)
+        def gathered(step, inside):
+            i = visit(step // chunks)
             j = peer(i)
+            c = step % chunks
 
             @pl.when((sec > 0) | (i > 0))
             def _():
                 remote(
-                    share.at[m], xin.at[m, j], x_s.at[m, j], x_r.at[m, j], sec, j
+                    share.at[m, :, in_cols(c)], xin.at[m, j, :, in_cols(c)],
+                    x_s.at[m, j, c], x_r.at[m, j, c], sec, j,
                 ).wait_recv()
 
             if relayed:
 
                 @pl.when((i == n - 2) & inner_chip)
                 def _():
-                    on_x(m, j).start()
-
-            piece = xin[m, j].astype(f32)
+                    on_x(m, j, c).start()
+
+            piece = xin[m, j, :, in_cols(c)].astype(f32)
             sq[...] += jnp.sum(piece * piece, axis=1, keepdims=True)
-            cols = pl.ds(pl.multiple_of(j * width, width), width)
-            scaled = (piece * gain[:, cols]).astype(bf16)
-            rows = pl.ds(pl.multiple_of(j * width, width), width)
+            rows = pl.ds(pl.multiple_of(j * width + c * in_half, in_half), in_half)
+            scaled = (piece * gain[:, rows]).astype(bf16)
             for at, w in enumerate((wq, wk, wv)):
                 raw[m, :, at * inner : (at + 1) * inner] += dot_nn(scaled, w[rows, :])
             return inside
 
-        lax.fori_loop(0, n, gathered, 0)
+        lax.fori_loop(0, n * chunks, gathered, 0)
         inv = lax.rsqrt(sq[:, :1] / model_width + epsilon)
         inv_kept[m] = jnp.broadcast_to(inv, (seq, 128))
         proj[m] = (raw[m] * inv).astype(bf16)
@@ -270,11 +314,13 @@
             prob = grown / jnp.sum(grown, axis=-1, keepdims=True)
             probs[m, p] = prob
             mixg[m, me, :, cols] = fold(dot_nn(prob.astype(bf16), v)).astype(bf16)
-
-        @pl.when(sec < sections - 1)
-        def _():
-            for i in range(n - 1, 0, -1):
-                unless_far(i, lambda i=i: mix_copy(m, peer(i)).start())
+            if (p + 1) % (groups // chunks) == 0:
+                c = p // (groups // chunks)
+
+                @pl.when(sec < sections - 1)
+                def _():
+                    for i in range(n - 1, 0, -1):
+                        unless_far(i, lambda i=i: mix_copy(m, peer(i), c).start())
 
         @pl.when(is_first & (m + 1 < micro))
         def _():
@@ -291,15 +337,11 @@
 
                 @pl.when(i > 0)
                 def _():
-                    remote(
-                        mixg.at[m, j], mixg.at[m, j], m_s.at[m, j], m_r.at[m, j], sec, j
-                    ).wait_recv()
-
-                if relayed:
-
-                    @pl.when((i == n - 2) & inner_chip)
-                    def _():
-                        on_mix(m, j).start()
+                    for c in range(chunks):
+                        part = mixg.at[m, j, :, mix_cols(c)]
+                        remote(part, part, m_s.at[m, j, c], m_r.at[m, j, c], sec, j).wait_recv()
+                        if relayed:
+                            pl.when((i == n - 2) & inner_chip)(on_mix(m, j, c).start)
 
                 rows = pl.ds(pl.multiple_of(j * inner, inner), inner)
                 acc[...] += dot_nn(mixg[m, j], wo[rows, :])
@@ -307,11 +349,15 @@
 
             lax.fori_loop(0, n, mixed, 0)
             share[m] = acc[...].astype(bf16)
-            for i in range(n - 1, -1, -1):
-                unless_far(i, lambda i=i: y_copy(m, peer(i)).start())
-
-    def i_copy(m, j):
-        return remote(ins.at[m, j], ip.at[m, me], i_s.at[m, j], i_r.at[m, me], sec, j)
+            for c in range(chunks):
+                for i in range(n - 1, -1, -1):
+                    unless_far(i, lambda i=i, c=c: y_copy(m, peer(i), c).start())
+
+    def i_copy(m, j, c):
+        return remote(
+            ins.at[m, j, :, in_cols(c)], ip.at[m, me, :, in_cols(c)],
+            i_s.at[m, j, c], i_r.at[m, me, c], sec, j,
+        )
 
     def r_copy(m, j):
         return remote(rads.at[m], rad.at[m, me], r_s.at[m, j], r_r.at[m, me], sec, j)
@@ -336,6 +382,7 @@
         )
 
     def receive(m):
+        pl.when((m == 0) & ~flips_first)(flip_all)
         g_copy(m, sec + 1).wait_recv()
         head_parts(m, gin)
 
@@ -350,7 +397,11 @@
             j = peer(i)
 
             def add():
-                remote(hs.at[m, j], hp.at[m, j], h_s.at[m, j], h_r.at[m, j], sec, j).wait_recv()
+                for c in range(chunks):
+                    remote(
+                        hs.at[m, j, :, mix_cols(c)], hp.at[m, j, :, mix_cols(c)],
+                        h_s.at[m, j, c], h_r.at[m, j, c], sec, j,
+                    ).wait_recv()
                 mg_ref[...] += hp[m, j].astype(f32)
 
             unless_far(i, add)
@@ -390,16 +441,16 @@
             r_copy(m, peer(i)).start()
 
         def input_part(step, inside):
-            i = emit(step)
-            j = peer(i)
-            rows = pl.ds(pl.multiple_of(j * width, width), width)
-            part = dot_nt(sgr[:, :inner], wq[rows, :])
-            part += dot_nt(sgr[:, inner : 2 * inner], wk[rows, :])
-            part += dot_nt(sgr[:, 2 * inner :], wv[rows, :])
-            pass_on(m, i, part, ins, ex_i, i_s, ei_r, i_copy)
+            i = emit(step // chunks)
+            c = step % chunks
+            at = pl.ds(pl.multiple_of(peer(i) * width + c * in_half, in_half), in_half)
+            part = dot_nn(sgr[:, :inner], wq_t[:, at])
+            part += dot_nn(sgr[:, inner : 2 * inner], wk_t[:, at])
+            part += dot_nn(sgr[:, 2 * inner :], wv_t[:, at])
+            pass_on(m, i, c, in_cols(c), part, ins, ex_i, i_s, ei_r, i_copy)
             return inside
 
-        lax.fori_loop(0, n, input_part, 0)
+        lax.fori_loop(0, n * chunks, input_part, 0)
 
         @pl.when(m == micro - 1)
         def _():
@@ -424,7 +475,11 @@
             sq[:8, :seq] += rad[m, j]
 
             def add():
-                remote(ins.at[m, j], ip.at[m, j], i_s.at[m, j], i_r.at[m, j], sec, j).wait_recv()
+                for c in range(chunks):
+                    remote(
+                        ins.at[m, j, :, in_cols(c)], ip.at[m, j, :, in_cols(c)],
+                        i_s.at[m, j, c], i_r.at[m, j, c], sec, j,
+                    ).wait_recv()
                 acc[...] += ip[m, j].astype(f32)
 
             unless_far(i, add)
@@ -467,30 +522,27 @@
     def finish(m, carry):
         def one(i, inside):
             j = peer(i)
-            h_copy(m, j).wait_send()
-            i_copy(m, j).wait_send()
             r_copy(m, j).wait_send()
-
-            @pl.when(is_first)
-            def _():
-                unless_far(i, lambda: x_copy(m, j).wait_send())
-
-            @pl.when(sec < sections - 1)
-            def _():
-                unless_far(i, lambda: mix_copy(m, j).wait_send())
+            for c in range(chunks):
+                h_copy(m, j, c).wait_send()
+                i_copy(m, j, c).wait_send()
+
+                @pl.when(is_first)
+                def _():
+                    unless_far(i, x_copy(m, j, c).wait_send)
+
+                @pl.when(sec < sections - 1)
+                def _():
+                    unless_far(i, mix_copy(m, j, c).wait_send)
 
             return inside
 
         lax.fori_loop(1, n, one, 0)
         if relayed:
 
-            @pl.when(inner_chip)
-            def _():
-                on_x(m, peer(n - 2)).wait_send()
-
-            @pl.when(inner_chip & (sec < sections - 1))
-            def _():
-                on_mix(m, peer(n - 2)).wait_send()
+            for c in range(chunks):
+                pl.when(inner_chip)(on_x(m, peer(n - 2), c).wait_send)
+                pl.when(inner_chip & (sec < sections - 1))(on_mix(m, peer(n - 2), c).wait_send)
 
         @pl.when(sec > 0)
         def _():
@@ -504,7 +556,8 @@
     def _():
         def one(m, carry):
             for i in range(n):
-                unless_far(i, lambda i=i: y_copy(m, peer(i)).wait_send())
+                for c in range(chunks):
+                    unless_far(i, y_copy(m, peer(i), c).wait_send)
             return carry
 
         lax.fori_loop(0, micro, one, 0)
@@ -540,6 +593,12 @@
     for at in range(1, dps):
         total = total + gains[at]
     gain_out[...] = total
+
+
+def hand_on(grads, gains, table, grads_out, gains_out, table_out):
+    grads_out[...] = grads[...]
+    gains_out[...] = gains[...]
+    table_out[...] = table[...]
 
 
 def per_device(
@@ -572,6 +631,10 @@
             pltpu.VMEM(w_key.shape[1:], bf16),
             pltpu.VMEM(w_value.shape[1:], bf16),
             pltpu.VMEM(w_out.shape[1:], bf16),
+            pltpu.VMEM(w_query.shape[:0:-1], bf16),
+            pltpu.VMEM(w_key.shape[:0:-1], bf16),
+            pltpu.VMEM(w_value.shape[:0:-1], bf16),
+            pltpu.VMEM(w_out.shape[:0:-1], bf16),
             pltpu.VMEM((heads, seq, seq), f32),
             pltpu.VMEM((micro, n, seq, width), bf16),
             pltpu.VMEM((micro, n, seq, inner), bf16),
@@ -600,17 +663,28 @@
             dma((4,)),
             dma((micro,)),
         ]
-        + [dma((micro, n))] * 11
+        + [dma((micro, n, 2))] * 9
+        + [dma((micro, n))] * 2
         + [dma((micro,))] * 2
         + [dma((sections * dps,))] * 2
         + [dma((dps,))] * 2
-        + [dma((micro,))] * 4,
+        + [dma((micro, 2))] * 4,
         compiler_params=pltpu.CompilerParams(
             collective_id=0, has_side_effects=True, vmem_limit_bytes=60 * 1024 * 1024
         ),
     )(
         stream, cotangent, token_ids, buckets, bias_table.T, gain, w_query, w_key, w_value, w_out,
     )
+    grads, gains, table_grad = pl.pallas_call(
+        hand_on,
+        out_shape=(
+            jax.ShapeDtypeStruct(grads.shape, bf16),
+            jax.ShapeDtypeStruct(gains.shape, f32),
+            jax.ShapeDtypeStruct(table_grad.shape, f32),
+        ),
+        in_specs=[vmem] * 3,
+        out_specs=(vmem,) * 3,
+    )(grads, gains, table_grad)
     return grads, gains, table_grad.T
 
 

time: 197 us -> 185 us (0.939)
  Pallas kernels: 191 us -> 185 us
  local copies, waits for them, and re-layouts: 4.22 us -> 0 us
    pallas_call x1, Pallas kernels: 191 us -> 183 us  [per_device(): pl.pallas_call(functools.partial(relay_kernel, sections, n, dps, head_dim...]
    unnamed x3 -> x0, local copies, waits for them, and re-layouts: 4.22 us -> none
where the time goes in v2:
time: 185 us
  Pallas kernels  185 us (100%)
    pallas_call x1, Pallas kernels, per_device(): pl.pallas_call(functools.partial(relay_kernel, sections, n, dps, head_dim...  183 us

profile of v2, /device:TPU:0, one launch (start us, length us, event | category | flops | bytes accessed | tf_op | source)
XLA Modules:
  0.0 185.3 jit_solution(4069750895688674868)
XLA Ops:
  0.6 183.0 %shard_map.121 = (bf16[1,2,64,1024]{3,2,1,0:T(8,128)(2,1)}, f32[1,1024]{1,0:T(1,128)}, f32[8,32]{1,0:T(8,128)}) custom-call(bf16[2,64,1024]{2,1,0:T(8,128)(2,1)} %stream.1, bf16[2,64,1024]{2,1,0:T(8,128)(2,1)} %cotangent.1, s32[2,64]{1,0:T(2,128)} %tokens.1, s32[64,64]{1,0:T(8,128)} %buckets.1, f32[8,32]{1,0:T(8,128)} %bitcast.2, f32[1,4096]{1,0:T(1,128)} %gain.1, ...), custom_call_target="tpu_custom_call" | custom-call | tf_op jit(solution)/shard_map/pallas_call | solution.py:619
  183.6 1.7 shard_map.122

commit v3 on v2

--- a/solution.py
+++ b/solution.py
@@ -32,9 +32,9 @@
     sections, n, dps, head_dim,
     stream, cotangent, tokens, buckets, table, gain, wq_hbm, wk_hbm, wv_hbm, wo_hbm,
     grads_out, gain_out, table_out,
-    wq, wk, wv, wo, wq_t, wk_t, wv_t, wo_t, bias, xin, mixg, hp, ip, rad, gin, hs, ins, rads, share, grad,
+    wq, wk, wv, wo, wq_t, wk_t, wv_t, wo_t, bias, xin, mixg, hp, ip, rad, gin, hs, ins, rads, share, grad, up, gain_own, gain_n, gains_n,
     raw, proj, probs, inv_kept, acc, mg_ref, sgr, sq, diag, tab, gains, ex_h, ex_i,
-    w_sem, l_sem, x_s, y_s, x_r, m_s, m_r, h_s, h_r, i_s, i_r, r_s, r_r, g_s, g_r, t_s, t_r, d_s, d_r, fx_s, fm_s, eh_r, ei_r,
+    w_sem, l_sem, x_s, y_s, x_r, m_s, m_r, h_s, h_r, i_s, i_r, r_s, r_r, b_s, b_r, u_s, u_r, q_s, q_r, e_s, t_s, t_r, d_s, d_r, fx_s, fm_s, eh_r, ei_r,
 ):
     micro, seq, width = stream.shape
     heads = bias.shape[0]
@@ -138,6 +138,20 @@
     greeters = n - 1 + everyone - 1 + n * jnp.minimum(sec, 1) + n * jnp.minimum(sections - 1 - sec, 1)
     pl.semaphore_wait(barrier, greeters)
 
+    above = jnp.maximum(sec - 1, 0)
+    bank = jnp.minimum(sec, 1)
+
+    def q_copy():
+        return remote(gain_own, gain_n, q_s.at[0], q_r.at[0], above, me)
+
+    gain_own[...] = gain[:, pl.ds(pl.multiple_of(me * width, width), width)]
+    pl.when(sec > 0)(lambda: q_copy().start())
+    gains_n[...] = jnp.zeros(gains_n.shape, f32)
+
+    @pl.when(sec == sections - 2)
+    def _():
+        up[...] = cotangent[...]
+
     def x_copy(m, j, c):
         return remote(
             stream.at[m, :, in_cols(c)], xin.at[m, me, :, in_cols(c)],
@@ -189,11 +203,11 @@
     def emit(at):
         return jnp.where(at == 0, 3, jnp.where(at == 3, 2, 2 - at)) if relayed else n - 1 - at
 
-    def pass_on(m, i, c, cols, part, own, extra, own_sem, extra_sem, copy):
+    def pass_on(m, i, c, cols, part, own, extra, own_sem, extra_sem, copy, lifted):
         j = peer(i)
         own[m, j, :, cols] = part.astype(bf16)
         if not relayed:
-            pl.when(i > 0)(lambda: copy(m, j, c).start())
+            pl.when((i > 0) | lifted)(lambda: copy(m, j, c).start())
             return
 
         def hand_over():
@@ -207,7 +221,7 @@
             hand_over().wait_recv()
             own[m, j, :, cols] = (part + extra[m, :, cols].astype(f32)).astype(bf16)
 
-        @pl.when((i > 0) & ((i < n - 1) | inner_chip))
+        @pl.when(((i > 0) | lifted) & ((i < n - 1) | inner_chip))
         def _():
             copy(m, j, c).start()
 
@@ -223,7 +237,7 @@
             part = dot_nn(upstream[m], wo_t[:, cols])
             for c in range(chunks):
                 at = slice(c * mix_half, (c + 1) * mix_half)
-                pass_on(m, i, c, at, part[:, at], hs, ex_h, h_s, eh_r, h_copy)
+                pass_on(m, i, c, at, part[:, at], hs, ex_h, h_s, eh_r, h_copy, False)
             return carry
 
         lax.fori_loop(0, n, one, 0)
@@ -355,15 +369,20 @@
 
     def i_copy(m, j, c):
         return remote(
-            ins.at[m, j, :, in_cols(c)], ip.at[m, me, :, in_cols(c)],
-            i_s.at[m, j, c], i_r.at[m, me, c], sec, j,
+            ins.at[m, j, :, in_cols(c)], ip.at[bank, m, me, :, in_cols(c)],
+            i_s.at[m, j, c], i_r.at[bank, m, me, c], above, j,
         )
 
     def r_copy(m, j):
-        return remote(rads.at[m], rad.at[m, me], r_s.at[m, j], r_r.at[m, me], sec, j)
-
-    def g_copy(m, to_sec):
-        return remote(grad.at[m], gin.at[m], g_s.at[m], g_r.at[m], to_sec, me)
+        return remote(
+            rads.at[m], rad.at[bank, m, me], r_s.at[m, j], r_r.at[bank, m, me], above, j
+        )
+
+    def back_copy(m):
+        return remote(gin.at[m], grad.at[m], b_s.at[m], b_r.at[m], sec + 1, me)
+
+    def up_copy(m):
+        return remote(gin.at[m], up.at[m], u_s.at[m], u_r.at[m], above, me)
 
     def t_copy(i):
         other = member(i)
@@ -381,16 +400,70 @@
             device_id={"dp": other}, device_id_type=MESH,
         )
 
+    def e_copy(other):
+        return pltpu.make_async_remote_copy(
+            src_ref=gains_n, dst_ref=gains.at[dp], send_sem=e_s.at[other], recv_sem=d_r.at[dp],
+            device_id={"section": sec + 1, "dp": other}, device_id_type=MESH,
+        )
+
+    def combine(m, deep, upstream, rows, gain_part):
+        if deep:
+            acc[...] = jnp.zeros(acc.shape, f32)
+            sq[:8, :seq] = jnp.zeros((8, seq), f32)
+        else:
+            acc[...] = ins[m, me].astype(f32)
+            sq[:8, :seq] = rads[m]
+
+        def arrived_input(i, inside):
+            j = peer(i)
+            remote(
+                rads.at[m], rad.at[deep, m, j], r_s.at[m, j], r_r.at[deep, m, j], sec, j
+            ).wait_recv()
+            sq[:8, :seq] += rad[deep, m, j]
+
+            def add():
+                for c in range(chunks):
+                    remote(
+                        ins.at[m, j, :, in_cols(c)], ip.at[deep, m, j, :, in_cols(c)],
+                        i_s.at[m, j, c], i_r.at[deep, m, j, c], sec, j,
+                    ).wait_recv()
+                acc[...] += ip[deep, m, j].astype(f32)
+
+            unless_far(i, add)
+            return inside
+
+        lax.fori_loop(1 - deep, n, arrived_input, 0)
+        inv = rad[1, m, me, 1:2, :] if deep else rads[m, 1:2, :]
+        weight = sq[:1, :seq] * inv * inv * inv / model_width
+        weight = jnp.broadcast_to(weight, (128, seq)).T[:, :1]
+        rows_f32 = rows.astype(f32)
+        normed = acc[...]
+        result = (upstream.astype(f32) + normed * gain_part - weight * rows_f32).astype(bf16)
+        return result, jnp.sum(normed * rows_f32, axis=0, keepdims=True)
+
     def receive(m):
-        pl.when((m == 0) & ~flips_first)(flip_all)
-        g_copy(m, sec + 1).wait_recv()
+        @pl.when(m == 0)
+        def _():
+            pl.when(~flips_first)(flip_all)
+            remote(gain_own, gain_n, q_s.at[0], q_r.at[0], sec, me).wait_recv()
+
+        @pl.when(sec < sections - 2)
+        def _():
+            remote(gin.at[m], up.at[m], u_s.at[m], u_r.at[m], sec, me).wait_recv()
+
+        result, part = combine(m, 1, up[m], share[m], gain_n[...])
+        gin[m] = result
         head_parts(m, gin)
+        back_copy(m).start()
+        pl.when(sec > 0)(lambda: up_copy(m).start())
+        gains_n[...] += part
+
+        @pl.when(m == micro - 1)
+        def _():
+            for other in range(dps):
+                e_copy(other).start()
 
     def backward(m):
-        @pl.when(is_last)
-        def _():
-            gin[m] = cotangent[m]
-
         mg_ref[...] = hs[m, me].astype(f32)
 
         def arrived(i, inside):
@@ -436,9 +509,10 @@
             for cols, part in ((q_cols, query_grad), (k_cols, key_grad), (v_cols, value_grad)):
                 radial = radial + part * raw[m, :, cols]
                 sgr[:, cols] = (part * inv).astype(bf16)
-        rads[m] = jnp.broadcast_to(jnp.sum(radial, axis=1, keepdims=True), (seq, 128)).T[:8]
+        rads[m] = jnp.where(lane == 0, jnp.sum(radial, axis=1, keepdims=True), inv).T[:8]
         for i in range(n - 1, 0, -1):
             r_copy(m, peer(i)).start()
+        pl.when(sec > 0)(lambda: r_copy(m, me).start())
 
         def input_part(step, inside):
             i = emit(step // chunks)
@@ -447,7 +521,7 @@
             part = dot_nn(sgr[:, :inner], wq_t[:, at])
             part += dot_nn(sgr[:, inner : 2 * inner], wk_t[:, at])
             part += dot_nn(sgr[:, 2 * inner :], wv_t[:, at])
-            pass_on(m, i, c, in_cols(c), part, ins, ex_i, i_s, ei_r, i_copy)
+            pass_on(m, i, c, in_cols(c), part, ins, ex_i, i_s, ei_r, i_copy, sec > 0)
             return inside
 
         lax.fori_loop(0, n * chunks, input_part, 0)
@@ -465,50 +539,18 @@
                 t_copy(i).start()
 
     def settle(m):
-        inv = inv_kept[m][:, :1]
-        acc[...] = ins[m, me].astype(f32)
-        sq[:8, :seq] = rads[m]
-
-        def arrived_input(i, inside):
-            j = peer(i)
-            remote(rads.at[m], rad.at[m, j], r_s.at[m, j], r_r.at[m, j], sec, j).wait_recv()
-            sq[:8, :seq] += rad[m, j]
-
-            def add():
-                for c in range(chunks):
-                    remote(
-                        ins.at[m, j, :, in_cols(c)], ip.at[m, j, :, in_cols(c)],
-                        i_s.at[m, j, c], i_r.at[m, j, c], sec, j,
-                    ).wait_recv()
-                acc[...] += ip[m, j].astype(f32)
-
-            unless_far(i, add)
-            return inside
-
-        lax.fori_loop(1, n, arrived_input, 0)
-        radial_sum = jnp.broadcast_to(sq[:1, :seq], (128, seq)).T[:, :1]
-        rows_f32 = xin[m, me].astype(f32)
-        normed = acc[...]
-        gain_own = gain[:, pl.ds(pl.multiple_of(me * width, width), width)]
-        weight = radial_sum * inv * inv * inv / model_width
-        result = (gin[m].astype(f32) + normed * gain_own - weight * rows_f32).astype(bf16)
-        grad[m] = result
+        result, part = combine(m, 0, gin[m], xin[m, me], gain_own[...])
         grads_out[0, m] = result
-
-        @pl.when(sec > 0)
-        def _():
-            g_copy(m, sec - 1).start()
-
-        gains[dp] += jnp.sum(normed * rows_f32, axis=0, keepdims=True)
+        gains[dp] += part
 
     def step(t, carry):
         u = t - 2 * micro
-        kind = jnp.where(u < 0, t % 2, u % 3 + 2)
-        m = jnp.where(u < 0, t // 2, u // 3)
-        of_last = t % 3
-        kind = jnp.where(is_last, jnp.where(of_last == 0, 0, of_last + 2), kind)
-        m = jnp.where(is_last, t // 3, m)
-        busy = ~is_last | (t < 3 * micro)
+        v = t - 4 * micro
+        kind = jnp.where(u < 0, t % 2, jnp.where(v < 0, u % 2 + 2, 4))
+        m = jnp.where(u < 0, t // 2, jnp.where(v < 0, u // 2, v))
+        kind = jnp.where(is_last, t % 2 * 3, kind)
+        m = jnp.where(is_last, t // 2, m)
+        busy = (t < 4 * micro) & (~is_last | (t < 2 * micro)) | is_first
 
         for at, act in enumerate((forward, project, receive, backward, settle)):
             pl.when((kind == at) & busy)(lambda act=act: act(m))
@@ -516,8 +558,29 @@
         return carry
 
     lax.fori_loop(0, 5 * micro, step, 0)
-    for i in range(1, dps):
-        d_copy(i).start()
+
+    @pl.when(is_first)
+    def _():
+        for i in range(1, dps):
+            d_copy(i).start()
+
+    @pl.when(sec > 0)
+    def _():
+        q_copy().wait_send()
+        for m in range(micro):
+            remote(gin.at[m], grad.at[m], b_s.at[m], b_r.at[m], sec, me).wait_recv()
+            grads_out[0, m] = grad[m]
+            r_copy(m, me).wait_send()
+            for c in range(chunks):
+                i_copy(m, me, c).wait_send()
+
+    @pl.when(sec < sections - 1)
+    def _():
+        for m in range(micro):
+            back_copy(m).wait_send()
+            pl.when(sec > 0)(up_copy(m).wait_send)
+        for other in range(dps):
+            e_copy(other).wait_send()
 
     def finish(m, carry):
         def one(i, inside):
@@ -543,10 +606,6 @@
             for c in range(chunks):
                 pl.when(inner_chip)(on_x(m, peer(n - 2), c).wait_send)
                 pl.when(inner_chip & (sec < sections - 1))(on_mix(m, peer(n - 2), c).wait_send)
-
-        @pl.when(sec > 0)
-        def _():
-            g_copy(m, sec - 1).wait_send()
 
         return carry
 
@@ -582,13 +641,18 @@
         part = jnp.sum(jnp.where(place == c, total, 0.0), axis=1, keepdims=True)
         summed = jnp.where(lane == c, part, summed)
     table_out[...] = summed[:heads, : table_out.shape[1]]
-    for i in range(1, dps):
-        other = (dp + i) % dps
-        pltpu.make_async_remote_copy(
+    def gain_in(other):
+        return pltpu.make_async_remote_copy(
             src_ref=gains.at[dp], dst_ref=gains.at[other],
             send_sem=d_s.at[other], recv_sem=d_r.at[other],
             device_id={"dp": other}, device_id_type=MESH,
-        ).wait()
+        )
+
+    for i in range(1, dps):
+        other = (dp + i) % dps
+        gain_in(other).wait_recv()
+        pl.when(is_first)(gain_in(other).wait_send)
+    pl.when(sec > 0)(gain_in(dp).wait_recv)
     total = gains[0]
     for at in range(1, dps):
         total = total + gains[at]
@@ -639,14 +703,18 @@
             pltpu.VMEM((micro, n, seq, width), bf16),
             pltpu.VMEM((micro, n, seq, inner), bf16),
             pltpu.VMEM((micro, n, seq, inner), bf16),
-            pltpu.VMEM((micro, n, seq, width), bf16),
-            pltpu.VMEM((micro, n, 8, seq), f32),
+            pltpu.VMEM((2, micro, n, seq, width), bf16),
+            pltpu.VMEM((2, micro, n, 8, seq), f32),
             pltpu.VMEM((micro, seq, width), bf16),
             pltpu.VMEM((micro, n, seq, inner), bf16),
             pltpu.VMEM((micro, n, seq, width), bf16),
             pltpu.VMEM((micro, 8, seq), f32),
             pltpu.VMEM((micro, seq, width), bf16),
             pltpu.VMEM((micro, seq, width), bf16),
+            pltpu.VMEM((micro, seq, width), bf16),
+            pltpu.VMEM((1, width), f32),
+            pltpu.VMEM((1, width), f32),
+            pltpu.VMEM((1, width), f32),
             pltpu.VMEM((micro, seq, 3 * inner), f32),
             pltpu.VMEM((micro, seq, 3 * inner), bf16),
             pltpu.VMEM((micro, groups, per * seq, seq), f32),
@@ -663,9 +731,11 @@
             dma((4,)),
             dma((micro,)),
         ]
-        + [dma((micro, n, 2))] * 9
-        + [dma((micro, n))] * 2
-        + [dma((micro,))] * 2
+        + [dma((micro, n, 2))] * 8
+        + [dma((2, micro, n, 2)), dma((micro, n)), dma((2, micro, n))]
+        + [dma((micro,))] * 4
+        + [dma((1,))] * 2
+        + [dma((dps,))]
         + [dma((sections * dps,))] * 2
         + [dma((dps,))] * 2
         + [dma((micro, 2))] * 4,

time: 185 us -> 181 us (0.978)
  Pallas kernels: 185 us -> 180 us
    pallas_call x1, Pallas kernels: 183 us -> 178 us  [per_device(): pl.pallas_call(functools.partial(relay_kernel, sections, n, dps, head_dim...]
where the time goes in v3:
time: 181 us
  Pallas kernels  180 us (99%)
    pallas_call x1, Pallas kernels, per_device(): pl.pallas_call(functools.partial(relay_kernel, sections, n, dps, head_dim...  178 us

profile of v3, /device:TPU:0, one launch (start us, length us, event | category | flops | bytes accessed | tf_op | source)
XLA Modules:
  0.0 180.6 jit_solution(1686732912901168448)
XLA Ops:
  0.6 178.2 %shard_map.121 = (bf16[1,2,64,1024]{3,2,1,0:T(8,128)(2,1)}, f32[1,1024]{1,0:T(1,128)}, f32[8,32]{1,0:T(8,128)}) custom-call(bf16[2,64,1024]{2,1,0:T(8,128)(2,1)} %stream.1, bf16[2,64,1024]{2,1,0:T(8,128)(2,1)} %cotangent.1, s32[2,64]{1,0:T(2,128)} %tokens.1, s32[64,64]{1,0:T(8,128)} %buckets.1, f32[8,32]{1,0:T(8,128)} %bitcast.2, f32[1,4096]{1,0:T(1,128)} %gain.1, ...), custom_call_target="tpu_custom_call" | custom-call | tf_op jit(solution)/shard_map/pallas_call | solution.py:683
  178.9 1.7 shard_map.122

commit v4 on v3

--- a/solution.py
+++ b/solution.py
@@ -10,8 +10,11 @@
 neg_fill = -1000000000.0
 epsilon = 1e-06
 MESH = pl.DeviceIdType.MESH
-DELAY = 8000
+DELAY = 12000
 DELAYED = 1
+EARLY = True
+CHUNKS = 4
+TOKEN = 0
 f32 = jnp.float32
 bf16 = jnp.bfloat16
 
@@ -34,7 +37,7 @@
     grads_out, gain_out, table_out,
     wq, wk, wv, wo, wq_t, wk_t, wv_t, wo_t, bias, xin, mixg, hp, ip, rad, gin, hs, ins, rads, share, grad, up, gain_own, gain_n, gains_n,
     raw, proj, probs, inv_kept, acc, mg_ref, sgr, sq, diag, tab, gains, ex_h, ex_i,
-    w_sem, l_sem, x_s, y_s, x_r, m_s, m_r, h_s, h_r, i_s, i_r, r_s, r_r, b_s, b_r, u_s, u_r, q_s, q_r, e_s, t_s, t_r, d_s, d_r, fx_s, fm_s, eh_r, ei_r,
+    w_sem, l_sem, x_s, y_s, x_r, m_s, m_r, h_s, h_r, i_s, i_r, r_s, r_r, b_s, b_r, u_s, u_r, q_s, q_r, e_s, t_s, t_r, d_s, d_r, fx_s, fm_s, eh_r, ei_r, tok,
 ):
     micro, seq, width = stream.shape
     heads = bias.shape[0]
@@ -53,7 +56,7 @@
         return (me + i * turn + n) % n
 
     relayed = n == 4
-    chunks = 2 if relayed and inner % 256 == 0 and width % 256 == 0 else 1
+    chunks = CHUNKS if relayed and inner % 512 == 0 and width % 512 == 0 else 1
     in_half, mix_half = width // chunks, inner // chunks
 
     def in_cols(c):
@@ -164,6 +167,8 @@
             y_s.at[m, j, c], x_r.at[m, me, c], sec + 1, j,
         )
 
+    late_x = dp % 2 == 1
+
     def send_x(m):
         pltpu.make_async_copy(stream.at[m], xin.at[m, me], l_sem.at[m]).start()
         for c in range(chunks):
@@ -177,6 +182,9 @@
             pl.delay(DELAY)
 
         send_x(0)
+        if EARLY:
+            for m in range(1, micro):
+                pl.when(dp % 2 == 0)(functools.partial(send_x, m))
 
     def head_bias(h, carry):
         value = jnp.zeros((seq, seq), f32)
@@ -336,7 +344,7 @@
                     for i in range(n - 1, 0, -1):
                         unless_far(i, lambda i=i: mix_copy(m, peer(i), c).start())
 
-        @pl.when(is_first & (m + 1 < micro))
+        @pl.when(is_first & (m + 1 < micro) & (late_x if EARLY else True))
         def _():
             send_x(m + 1)
 
@@ -453,7 +461,10 @@
 
         result, part = combine(m, 1, up[m], share[m], gain_n[...])
         gin[m] = result
+        if TOKEN:
+            pl.when(dp % 2 == 1)(lambda: pl.semaphore_wait(tok.at[m], 1))
         head_parts(m, gin)
+        pass_token(m, 3)
         back_copy(m).start()
         pl.when(sec > 0)(lambda: up_copy(m).start())
         gains_n[...] += part
@@ -462,6 +473,15 @@
         def _():
             for other in range(dps):
                 e_copy(other).start()
+
+    def pass_token(m, at):
+        if TOKEN == at:
+
+            @pl.when((dp % 2 == 0) & (dp + 1 < dps) & (sec < sections - 1))
+            def _():
+                pl.semaphore_signal(
+                    tok.at[m], inc=1, device_id={"dp": dp + 1}, device_id_type=MESH
+                )
 
     def backward(m):
         mg_ref[...] = hs[m, me].astype(f32)
@@ -481,6 +501,7 @@
             return inside
 
         lax.fori_loop(1, n, arrived, 0)
+        pass_token(m, 1)
         inv = inv_kept[m][:, :1]
         radial = jnp.zeros((seq, 128), f32)
         for p in range(groups):
@@ -525,6 +546,7 @@
             return inside
 
         lax.fori_loop(0, n * chunks, input_part, 0)
+        pass_token(m, 2)
 
         @pl.when(m == micro - 1)
         def _():
@@ -538,7 +560,29 @@
             for i in range(1, everyone):
                 t_copy(i).start()
 
+    def finish_table():
+        def table_wait(i, carry):
+            other = member(i)
+            pltpu.make_async_remote_copy(
+                src_ref=tab.at[mine], dst_ref=tab.at[other],
+                send_sem=t_s.at[other], recv_sem=t_r.at[other],
+                device_id={"section": other // dps, "dp": other % dps}, device_id_type=MESH,
+            ).wait()
+            return carry
+
+        lax.fori_loop(1, everyone, table_wait, 0)
+        total = tab[0]
+        for at in range(1, everyone):
+            total = total + tab[at]
+        last = buckets[seq - 1 : seq, :]
+        place = jnp.concatenate([buckets[0:1, :], last[:, seq - 1 :], last[:, : seq - 1]], axis=1)
+        summed = jnp.zeros(total.shape, f32)
+        for c in range(table.shape[1]):
+            part = jnp.sum(jnp.where(place == c, total, 0.0), axis=1, keepdims=True)
+            summed = jnp.where(lane == c, part, summed)
+        table_out[...] = summed[:heads, : table_out.shape[1]]
     def settle(m):
+        pl.when(m == micro - 1)(finish_table)
         result, part = combine(m, 0, gin[m], xin[m, me], gain_own[...])
         grads_out[0, m] = result
         gains[dp] += part
@@ -621,26 +665,8 @@
 
         lax.fori_loop(0, micro, one, 0)
 
-    def table_wait(i, carry):
-        other = member(i)
-        pltpu.make_async_remote_copy(
-            src_ref=tab.at[mine], dst_ref=tab.at[other],
-            send_sem=t_s.at[other], recv_sem=t_r.at[other],
-            device_id={"section": other // dps, "dp": other % dps}, device_id_type=MESH,
-        ).wait()
-        return carry
-
-    lax.fori_loop(1, everyone, table_wait, 0)
-    total = tab[0]
-    for at in range(1, everyone):
-        total = total + tab[at]
-    last = buckets[seq - 1 : seq, :]
-    place = jnp.concatenate([buckets[0:1, :], last[:, seq - 1 :], last[:, : seq - 1]], axis=1)
-    summed = jnp.zeros(total.shape, f32)
-    for c in range(table.shape[1]):
-        part = jnp.sum(jnp.where(place == c, total, 0.0), axis=1, keepdims=True)
-        summed = jnp.where(lane == c, part, summed)
-    table_out[...] = summed[:heads, : table_out.shape[1]]
+    pl.when(sec > 0)(finish_table)
+
     def gain_in(other):
         return pltpu.make_async_remote_copy(
             src_ref=gains.at[dp], dst_ref=gains.at[other],
@@ -731,14 +757,15 @@
             dma((4,)),
             dma((micro,)),
         ]
-        + [dma((micro, n, 2))] * 8
-        + [dma((2, micro, n, 2)), dma((micro, n)), dma((2, micro, n))]
+        + [dma((micro, n, CHUNKS))] * 8
+        + [dma((2, micro, n, CHUNKS)), dma((micro, n)), dma((2, micro, n))]
         + [dma((micro,))] * 4
         + [dma((1,))] * 2
         + [dma((dps,))]
         + [dma((sections * dps,))] * 2
         + [dma((dps,))] * 2
-        + [dma((micro, 2))] * 4,
+        + [dma((micro, CHUNKS))] * 4
+        + [pltpu.SemaphoreType.REGULAR((micro,))],
         compiler_params=pltpu.CompilerParams(
             collective_id=0, has_side_effects=True, vmem_limit_bytes=60 * 1024 * 1024
         ),

time: 181 us -> 177 us (0.978)
  Pallas kernels: 180 us -> 176 us
    pallas_call x1, Pallas kernels: 178 us -> 174 us  [per_device(): pl.pallas_call(functools.partial(relay_kernel, sections, n, dps, head_dim...]
where the time goes in v4:
time: 177 us; the launch traced here: 176 us
  Pallas kernels  176 us (99%)
    pallas_call x1, Pallas kernels, per_device(): pl.pallas_call(functools.partial(relay_kernel, sections, n, dps, head_dim...  174 us

profile of v4, /device:TPU:0, one launch (start us, length us, event | category | flops | bytes accessed | tf_op | source)
XLA Modules:
  0.0 176.4 jit_solution(81745032632570992)
XLA Ops:
  0.6 174.1 %shard_map.121 = (bf16[1,2,64,1024]{3,2,1,0:T(8,128)(2,1)}, f32[1,1024]{1,0:T(1,128)}, f32[8,32]{1,0:T(8,128)}) custom-call(bf16[2,64,1024]{2,1,0:T(8,128)(2,1)} %stream.1, bf16[2,64,1024]{2,1,0:T(8,128)(2,1)} %cotangent.1, s32[2,64]{1,0:T(2,128)} %tokens.1, s32[64,64]{1,0:T(8,128)} %buckets.1, f32[8,32]{1,0:T(8,128)} %bitcast.2, f32[1,4096]{1,0:T(1,128)} %gain.1, ...), custom_call_target="tpu_custom_call" | custom-call | tf_op jit(solution)/shard_map/pallas_call | solution.py:709
  174.8 1.7 shard_map.122

commit v5 on v4

--- a/solution.py
+++ b/solution.py
@@ -465,7 +465,6 @@
             pl.when(dp % 2 == 1)(lambda: pl.semaphore_wait(tok.at[m], 1))
         head_parts(m, gin)
         pass_token(m, 3)
-        back_copy(m).start()
         pl.when(sec > 0)(lambda: up_copy(m).start())
         gains_n[...] += part
 
@@ -546,6 +545,7 @@
             return inside
 
         lax.fori_loop(0, n * chunks, input_part, 0)
+        pl.when(sec < sections - 1)(lambda: back_copy(m).start())
         pass_token(m, 2)
 
         @pl.when(m == micro - 1)

time: 177 us -> 176 us (level)
  no operation moved by 1% of the time
where the time goes in v5:
time: 176 us
  Pallas kernels  175 us (99%)
    pallas_call x1, Pallas kernels, per_device(): pl.pallas_call(functools.partial(relay_kernel, sections, n, dps, head_dim...  174 us

profile of v5, /device:TPU:0, one launch (start us, length us, event | category | flops | bytes accessed | tf_op | source)
XLA Modules:
  0.0 176.0 jit_solution(2124842228449030615)
XLA Ops:
  0.6 173.6 %shard_map.121 = (bf16[1,2,64,1024]{3,2,1,0:T(8,128)(2,1)}, f32[1,1024]{1,0:T(1,128)}, f32[8,32]{1,0:T(8,128)}) custom-call(bf16[2,64,1024]{2,1,0:T(8,128)(2,1)} %stream.1, bf16[2,64,1024]{2,1,0:T(8,128)(2,1)} %cotangent.1, s32[2,64]{1,0:T(2,128)} %tokens.1, s32[64,64]{1,0:T(8,128)} %buckets.1, f32[8,32]{1,0:T(8,128)} %bitcast.2, f32[1,4096]{1,0:T(1,128)} %gain.1, ...), custom_call_target="tpu_custom_call" | custom-call | tf_op jit(solution)/shard_map/pallas_call | solution.py:709
  174.3 1.7 shard_map.122
